TPU v7x, 32 devices: a whole 2x2x4 slice. The times are simulated.
32 devices in a mesh: outer: 4 (over y, x), dev: 8 (over z, core).
Axes of the slice: x: 2, y: 2, z: 4, core: 2. Of those that a mesh axis runs over, the one named last changes fastest.
Arguments:
- documents: bfloat16 [6144, 4096], P(('outer', 'dev')), may hold values from -8 to 8
- cluster_of: int32 [6144], replicated, may hold values from 0 to 31, as said below
- neighbours: int32 [32, 4], replicated, may hold values from 0 to 31, as said below
- sharpness: float32 [32], replicated, may hold values from 32 to 64
Outputs:
- density: float32 [6144], P(('outer', 'dev'))
Inputs may be any that keep to these rules, and one draw needn't show every extreme that they name: `cluster_of`: rows b * 192 to (b + 1) * 192 - 1 form block b. Block b names only clusters g * 8 to (g + 1) * 8 - 1, with g = b // 8, and names no cluster more than 48 times; in each group g some cluster is named exactly 48 times by every block of that group; every cluster is named by some row. `neighbours`: row c, with c = g * 8 + h, lists in order the clusters g * 8 + ((h - 1) mod 8), g * 8 + ((h + 1) mod 8), ((g - 1) mod 4) * 8 + ((h + b) mod 8) and ((g + 1) mod 4) * 8 + ((h + d) mod 8), with b and d each in -1, 0, 1.
All inputs are finite; a program needn't handle non-finite values.
Results may differ from a plain program's by a relative error of at most 0.00047.
Values may be sent and summed in bfloat16 or wider, within the bound.
A program may use at most 128 MiB of HBM per device.

v0:
```python
import math
import jax
import jax.numpy as jnp
from jax import lax
from jax.sharding import PartitionSpec as P


def passed_along(block, axis, distance):
    devices = range(lax.axis_size(axis))
    route = [((i - distance) % len(devices), i) for i in devices]
    return lax.ppermute(block, axis, route)


def kernel_block(queries, others, pair_gain):
    products = jnp.einsum("qe,ke->qk", queries, others, preferred_element_type=jnp.float32)
    return jnp.exp(pair_gain * products)


def shards(documents, cluster_of, neighbours, sharpness):
    groups = lax.axis_size("outer")
    owners = lax.axis_size("dev")
    tokens_here = documents.shape[0]
    feature_width = documents.shape[1]
    capacity = max(2, 2 * tokens_here // owners)
    slot_count = owners * capacity
    group_index = lax.axis_index("outer")
    owner_index = lax.axis_index("dev")
    own_cluster = group_index * owners + owner_index
    block_labels = cluster_of.reshape(groups * owners, tokens_here)
    group_of_block = jnp.arange(groups * owners, dtype=jnp.int32) // owners
    local_labels = block_labels - group_of_block[:, None] * owners
    owner_range = jnp.arange(owners, dtype=jnp.int32)
    per_block = jnp.sum(
        (local_labels[:, :, None] == owner_range).astype(jnp.int32), axis=1
    ).reshape(groups, owners, owners)
    cluster_sizes = jnp.sum(per_block, axis=1).reshape(-1)
    own_labels = lax.dynamic_index_in_dim(local_labels, own_cluster, 0, keepdims=False)
    ordinal = jnp.arange(tokens_here, dtype=jnp.int32)
    earlier = ordinal[None, :] < ordinal[:, None]
    repeats = jnp.sum(
        ((own_labels[:, None] == own_labels[None, :]) & earlier).astype(jnp.int32), axis=1
    )
    target = own_labels * capacity + repeats
    placing = (jnp.arange(slot_count, dtype=jnp.int32)[:, None] == target[None, :]).astype(
        jnp.bfloat16
    )
    outgoing = jnp.dot(placing, documents, preferred_element_type=jnp.float32).astype(jnp.bfloat16)
    arrived = lax.all_to_all(
        outgoing.reshape(owners, capacity, feature_width),
        "dev",
        split_axis=0,
        concat_axis=0,
        tiled=True,
    ).reshape(slot_count, feature_width)

    def slot_mask(group_at, owner_at):
        senders = per_block[group_at, :, owner_at]
        return (
            (jnp.arange(capacity, dtype=jnp.int32)[None, :] < senders[:, None])
            .astype(jnp.float32)
            .reshape(-1)
        )

    present = slot_mask(group_index, owner_index)
    centre = jnp.dot(
        present.astype(jnp.bfloat16)[None, :], arrived, preferred_element_type=jnp.float32
    )[0]
    centre = centre / cluster_sizes[own_cluster].astype(jnp.float32)
    centred = arrived.astype(jnp.float32) - centre[None, :]
    scaling = lax.rsqrt(jnp.mean(centred * centred, axis=1) + 1e-06) / math.sqrt(feature_width)
    unit_rows = (centred * (scaling * present)[:, None]).astype(jnp.bfloat16)
    own_gain = sharpness[own_cluster]
    listed = neighbours[own_cluster]
    off_diagonal = 1.0 - jnp.eye(slot_count, dtype=jnp.float32)
    running = jnp.sum(
        kernel_block(unit_rows, unit_rows, own_gain) * (present[None, :] * off_diagonal), axis=1
    )
    beside = [passed_along(unit_rows, "dev", offset) for offset in (1, -1)]
    vertical = []
    for direction, position in ((1, 2), (-1, 3)):
        receiver_group = (group_index + direction) % groups
        wanted = neighbours[receiver_group * owners + owner_index, position]
        delta = (wanted % owners - owner_index + owners) % owners
        picked_rows = jnp.where(
            delta == 1, beside[1], jnp.where(delta == owners - 1, beside[0], unit_rows)
        )
        vertical.append(passed_along(picked_rows, "outer", direction))
    key_sets = [beside[0], beside[1], vertical[0], vertical[1]]
    for position in range(4):
        partner = listed[position]
        partner_group_at = partner // owners
        partner_owner_at = partner % owners
        partner_partner = partner_group_at * owners + partner_owner_at
        pair_gain = 0.5 * (own_gain + sharpness[partner_partner])
        partner = partner_partner
        kernel_terms = kernel_block(unit_rows, key_sets[position], pair_gain)
        key_mask = slot_mask(partner_group_at, partner_owner_at)
        running = running + jnp.sum(kernel_terms * key_mask[None, :], axis=1)
    partner_count = cluster_sizes[own_cluster] - 1 + jnp.sum(cluster_sizes[listed])
    slot_density = jnp.log(running / partner_count.astype(jnp.float32))
    answered = lax.all_to_all(
        slot_density.reshape(owners, capacity), "dev", split_axis=0, concat_axis=0, tiled=True
    ).reshape(-1)
    return answered[target]


def lookup(table, index):
    hit = index[:, None] == jnp.arange(table.shape[0], dtype=jnp.int32)[None, :]
    return jnp.sum(jnp.where(hit, table[None, :], jnp.zeros((), table.dtype)), axis=1)


def gathered(documents, cluster_of, neighbours, sharpness):
    groups = lax.axis_size("outer")
    owners = lax.axis_size("dev")
    tokens_here, feature_width = documents.shape
    group_index = lax.axis_index("outer")
    owner_index = lax.axis_index("dev")
    clusters = groups * owners
    group_rows = owners * tokens_here
    cluster_range = jnp.arange(clusters, dtype=jnp.int32)
    sizes = jnp.sum((cluster_of[:, None] == cluster_range[None, :]).astype(jnp.int32), axis=0)

    def labels_at(group_at):
        start = (group_at * owners + owner_index) * tokens_here
        return lax.dynamic_slice_in_dim(cluster_of, start, tokens_here)

    previous = (group_index + groups - 1) % groups
    following = (group_index + 1) % groups
    own = labels_at(group_index)
    local = own - group_index * owners
    local_range = jnp.arange(owners, dtype=jnp.int32)
    member = (local_range[:, None] == local[None, :]).astype(jnp.bfloat16)
    sums = lax.psum(jnp.dot(member, documents, preferred_element_type=jnp.float32), "dev")
    own_sizes = lax.dynamic_slice_in_dim(sizes, group_index * owners, owners)
    means = sums / own_sizes.astype(jnp.float32)[:, None]
    centre = jnp.dot(
        member.astype(jnp.float32).T,
        means,
        precision=lax.Precision.HIGHEST,
        preferred_element_type=jnp.float32,
    )
    centred = documents.astype(jnp.float32) - centre
    scaling = lax.rsqrt(jnp.mean(centred * centred, axis=1) + 1e-06) / math.sqrt(feature_width)
    unit_rows = (centred * scaling[:, None]).astype(jnp.bfloat16)
    from_previous = passed_along(unit_rows, "outer", 1)
    from_following = passed_along(unit_rows, "outer", -1)
    keys = lax.all_gather(unit_rows, "dev", axis=0, tiled=True)
    key_labels = lax.dynamic_slice_in_dim(cluster_of, group_index * group_rows, group_rows)
    key_gain = lookup(sharpness, key_labels)

    def partial(queries, labels, positions, own_too):
        products = jnp.einsum("qe,ke->qk", queries, keys, preferred_element_type=jnp.float32)
        gain = 0.5 * (lookup(sharpness, labels)[:, None] + key_gain[None, :])
        wanted = jnp.zeros(products.shape, jnp.bool_)
        for position in positions:
            listed = lookup(neighbours[:, position], labels)
            wanted = wanted | (listed[:, None] == key_labels[None, :])
        if own_too:
            at = owner_index * tokens_here + jnp.arange(tokens_here, dtype=jnp.int32)
            other = at[:, None] != jnp.arange(group_rows, dtype=jnp.int32)[None, :]
            wanted = wanted | (labels[:, None] == key_labels[None, :]) & other
        return jnp.sum(jnp.where(wanted, jnp.exp(gain * products), 0.0), axis=1)

    back_previous = partial(from_previous, labels_at(previous), (3,), False)
    back_following = partial(from_following, labels_at(following), (2,), False)
    running = partial(unit_rows, own, (0, 1), True)
    running = running + passed_along(back_previous, "outer", -1)
    running = running + passed_along(back_following, "outer", 1)
    counts = sizes - 1
    for position in range(neighbours.shape[1]):
        counts = counts + lookup(sizes, neighbours[:, position])
    return jnp.log(running / lookup(counts, own).astype(jnp.float32))


def solution(mesh):
    small = mesh.shape["dev"] <= 8
    in_specs = (P(("outer", "dev"), None), P(), P(), P())
    out_specs = P(("outer", "dev"))
    body = gathered if small else shards
    return jax.shard_map(body, mesh=mesh, in_specs=in_specs, out_specs=out_specs, check_vma=False)
```

profile of v0, /device:TPU:0, one launch (start us, length us, event | category | flops | bytes accessed | tf_op | source)
XLA Modules:
  0.0 226.7 jit_solution(15810836763792392852)
XLA Ops:
  6.5 0.0 copy-start.2
  6.5 0.0 copy-start.1
  6.5 0.0 all-reduce.2.cloned.1.call-start
  6.5 0.9 broadcast_subtract_fusion
  7.5 2.4 %fusion.13 = f32[8,4096]{1,0:T(8,128)} fusion(bf16[192,4096]{1,0:T(8,128)(2,1)} %param.4, s32[192]{0:T(256)S(1)} %get-tuple-element.15), kind=kOutput, calls=%fused_computation.44 | convolution fusion | flops 12584448 | bytes 1704704 | tf_op jit(solution)/shard_map/dot_general | solution.py:133
  9.8 0.0 all-reduce.2.cloned.1.call-update
  9.9 0.0 all-gather.2.cloned.1.call-start
  9.9 0.0 copy-done.2
  9.9 0.2 convert_reduce_fusion
  10.1 0.1 dynamic-slice_convert_fusion
  10.2 57.5 %all-reduce.2.cloned.1.call-done = f32[8,4096]{1,0:T(8,128)} async-done(((f32[8,4096]{1,0:T(8,128)}), f32[8,4096]{1,0:T(8,128)}) %all-reduce.2.cloned.1.call-update) | async-done | bytes 131088 | tf_op jit(solution)/shard_map/psum | solution.py:133
  67.7 0.0 copy-done.1
  67.7 2.8 %multiply_reduce_fusion = (f32[192]{0:T(256)S(1)}, f32[192,4096]{1,0:T(8,128)S(1)}) fusion(f32[8,4096]{1,0:T(8,128)} %all-reduce.2.cloned.1.call-done, f32[8]{0:T(128)S(1)} %dynamic-slice_convert_fusion, s32[192]{0:T(256)S(1)} %get-tuple-element.15, bf16[192,4096]{1,0:T(8,128)(2,1)S(1)} %copy-done.1), kind=kOutput, calls=%fused_computation.2 | convolution fusion | flops 78677312 | bytes 4851232 | tf_op jit(solution)/shard_map/dot_general | solution.py:136
  70.5 1.5 multiply_convert_fusion
  72.0 0.0 copy-start
  72.0 0.0 copy-start.3
  72.0 0.0 copy-start.4
  72.0 0.0 all-gather.2.cloned.1.call-update
  72.1 1.4 copy-done
  73.4 2.4 %collective-permute-start.2 = (bf16[192,4096]{1,0:T(8,128)(2,1)S(1)}, bf16[192,4096]{1,0:T(8,128)(2,1)S(1)}, u32[]{:S(2)}, u32[]{:S(2)}) collective-permute-start(bf16[192,4096]{1,0:T(8,128)(2,1)S(1)} %copy-done), channel_id=1, source_target_pairs={{8,0},{16,8},{24,16},{0,24},{9,1},{17,9},{25,17},{1,25},{10,2},{18... | collective-permute-start | bytes 4718600 | tf_op jit(solution)/shard_map/ppermute | solution.py:11
  75.8 0.1 dynamic_slice.16
  75.9 0.0 copy-done.3
  75.9 0.1 select_reduce_fusion.3
  76.0 0.1 select_reduce_fusion.5
  76.1 0.0 copy-done.4
  76.1 0.1 select_reduce_fusion.4
  76.2 0.1 collective-permute-start
  76.3 0.2 select_reduce_fusion.12
  76.5 0.1 select_reduce_fusion.8
  76.6 0.1 select_reduce_fusion
  76.7 34.0 %collective-permute-done.2 = bf16[192,4096]{1,0:T(8,128)(2,1)S(1)} collective-permute-done((bf16[192,4096]{1,0:T(8,128)(2,1)S(1)}, bf16[192,4096]{1,0:T(8,128)(2,1)S(1)}, u32[]{:S(2)}, u32[]{:S(2)}) %collective-permute-start.2) | collective-permute-done | bytes 1572896 | tf_op jit(solution)/shard_map/ppermute | solution.py:11
  110.7 77.3 %all-gather.2.cloned.1.call-done = bf16[1536,4096]{1,0:T(8,128)(2,1)} async-done(((bf16[192,4096]{1,0:T(8,128)(2,1)}), bf16[1536,4096]{1,0:T(8,128)(2,1)}) %all-gather.2.cloned.1.call-update) | async-done | bytes 12582928 | tf_op jit(solution)/shard_map/all_gather | solution.py:147
  188.0 9.1 %fusion.8 = f32[192]{0:T(256)S(1)} fusion(bf16[192,4096]{1,0:T(8,128)(2,1)S(1)} %collective-permute-done.2, bf16[1536,4096]{1,0:T(8,128)(2,1)} %all-gather.2.cloned.1.call-done, f32[192]{0:T(256)S(1)} %get-tuple-element.9, f32[1536]{0:T(1024)S(1)} %select_reduce_fusion, s32[1536]{0:T(1024)S(1)} %dynamic_slice.16, s32[192]{0:T(256)S(1)} %select_reduce_fusion.3), kind=kOutput, calls=%fused_computation.14 | convolution fusion | flops 2417688320 | bytes 14170368 | tf_op jit(solution)/shard_map/qe,ke->qk/dot_general | solution.py:152
  197.1 1.5 collective-permute-start.3
  198.6 0.0 collective-permute-done
  198.6 9.6 %fusion.7 = f32[192]{0:T(256)S(1)} fusion(bf16[192,4096]{1,0:T(8,128)(2,1)} %collective-permute-done, bf16[1536,4096]{1,0:T(8,128)(2,1)} %all-gather.2.cloned.1.call-done, f32[192]{0:T(256)S(1)} %get-tuple-element.8, f32[1536]{0:T(1024)S(1)} %select_reduce_fusion, s32[1536]{0:T(1024)S(1)} %dynamic_slice.16, s32[192]{0:T(256)S(1)} %select_reduce_fusion.5), kind=kOutput, calls=%fused_computation.13 | convolution fusion | flops 2417688320 | bytes 14170368 | tf_op jit(solution)/shard_map/qe,ke->qk/dot_general | solution.py:152
  208.2 1.7 collective-permute-start.1
  209.9 9.4 %fusion.6 = f32[192]{0:T(256)S(1)} fusion(bf16[192,4096]{1,0:T(8,128)(2,1)S(1)} %copy-done, bf16[1536,4096]{1,0:T(8,128)(2,1)} %all-gather.2.cloned.1.call-done, f32[1536]{0:T(1024)S(1)} %select_reduce_fusion, f32[192]{0:T(256)S(1)} %get-tuple-element.10, s32[192]{0:T(256)S(1)} %iota_add_fusion, s32[1536]{0:T(1024)S(1)} %dynamic_slice.16, ...), kind=kOutput, calls=%fused_computation.12 | convolution fusion | flops 2419457792 | bytes 14172672 | tf_op jit(solution)/shard_map/qe,ke->qk/dot_general | solution.py:152
  219.3 0.0 collective-permute-done.3
  219.3 0.0 collective-permute-done.1
  219.3 0.6 fusion.16
  (4 shorter events, 0.0 us)
Async XLA Ops:
  6.5 3.4 %copy-start.2 = (s32[6144]{0:T(1024)S(1)}, s32[6144]{0:T(1024)}, u32[]{:S(2)}) copy-start(s32[6144]{0:T(1024)} %param.5) | copy-start | bytes 73732
  6.5 61.2 %copy-start.1 = (bf16[192,4096]{1,0:T(8,128)(2,1)S(1)}, bf16[192,4096]{1,0:T(8,128)(2,1)}, u32[]{:S(2)}) copy-start(bf16[192,4096]{1,0:T(8,128)(2,1)} %param.4) | copy-start | bytes 4718596
  6.5 61.2 %all-reduce.2.cloned.1.call-start = ((), (), s32[]{:S(2)}) async-start(), calls=%async_computation | async-start | bytes 262144 | tf_op jit(solution)/shard_map/psum | solution.py:133
  9.9 178.2 %all-gather.2.cloned.1.call-start = ((), (), s32[]{:S(2)}) async-start(), calls=%async_computation.1 | async-start | bytes 14155776 | tf_op jit(solution)/shard_map/all_gather | solution.py:147
  72.0 1.4 copy-start
  72.0 3.9 %copy-start.3 = (s32[32,4]{0,1:T(4,128)S(1)}, s32[32,4]{0,1:T(4,128)}, u32[]{:S(2)}) copy-start(s32[32,4]{0,1:T(4,128)} %param.6) | copy-start | bytes 1540
  72.0 4.0 %copy-start.4 = (f32[32]{0:T(128)S(1)}, f32[32]{0:T(128)}, u32[]{:S(2)}) copy-start(f32[32]{0:T(128)} %param.7) | copy-start | bytes 388
  73.4 37.3 %collective-permute-start.2 = (bf16[192,4096]{1,0:T(8,128)(2,1)S(1)}, bf16[192,4096]{1,0:T(8,128)(2,1)S(1)}, u32[]{:S(2)}, u32[]{:S(2)}) collective-permute-start(bf16[192,4096]{1,0:T(8,128)(2,1)S(1)} %copy-done), channel_id=1, source_target_pairs={{8,0},{16,8},{24,16},{0,24},{9,1},{17,9},{25,17},{1,25},{10,2},{18... | collective-permute-start | bytes 4718600 | tf_op jit(solution)/shard_map/ppermute | solution.py:11
  76.2 122.4 %collective-permute-start = (bf16[192,4096]{1,0:T(8,128)(2,1)S(1)}, bf16[192,4096]{1,0:T(8,128)(2,1)}, u32[]{:S(2)}, u32[]{:S(2)}) collective-permute-start(bf16[192,4096]{1,0:T(8,128)(2,1)S(1)} %copy-done), channel_id=1, source_target_pairs={{24,0},{0,8},{8,16},{16,24},{25,1},{1,9},{9,17},{17,25},{26,2},{2,... | collective-permute-start | bytes 4718600 | tf_op jit(solution)/shard_map/ppermute | solution.py:11
  197.1 22.2 %collective-permute-start.3 = (f32[192]{0:T(256)S(1)}, f32[192]{0:T(256)S(1)}, u32[]{:S(2)}, u32[]{:S(2)}) collective-permute-start(f32[192]{0:T(256)S(1)} %fusion.8), channel_id=1, source_target_pairs={{24,0},{0,8},{8,16},{16,24},{25,1},{1,9},{9,17},{17,25},{26,2},{2,... | collective-permute-start | bytes 2312 | tf_op jit(solution)/shard_map/ppermute | solution.py:11
  208.2 11.1 %collective-permute-start.1 = (f32[192]{0:T(256)S(1)}, f32[192]{0:T(256)S(1)}, u32[]{:S(2)}, u32[]{:S(2)}) collective-permute-start(f32[192]{0:T(256)S(1)} %fusion.7), channel_id=1, source_target_pairs={{8,0},{16,8},{24,16},{0,24},{9,1},{17,9},{25,17},{1,25},{10,2},{18... | collective-permute-start | bytes 2312 | tf_op jit(solution)/shard_map/ppermute | solution.py:11
Sparse Core Ops, SparseCore 0:
  10.0 57.6 all-reduce.1
  72.2 115.8 all-gather.1
where the time goes:
time: 227 us
  waiting for transfers between devices  169 us (74%)
  matrix products  33.2 us (15%)
  between operations  13.5 us (6%)
  starting transfers between devices  5.69 us (3%)
  other arithmetic  4.04 us (2%)
    all_gather x1, waiting for transfers between devices, gathered(): keys = lax.all_gather(unit_rows, 'dev', axis=0, tiled=True)  77.3 us
    psum x1, waiting for transfers between devices, gathered(): lax.psum(jnp.dot(member, documents, preferred_element_type=jnp.float32),...  57.5 us
    ppermute x4, waiting for transfers between devices, passed_along(): return lax.ppermute(block, axis, route)  34 us
    dot_general x3, matrix products, partial(): jnp.einsum('qe,ke->qk', queries, keys, preferred_element_type=jnp.float32)  28 us
    ppermute x4, starting transfers between devices, passed_along(): return lax.ppermute(block, axis, route)  5.65 us
  transfers between devices with their start and end apart: 6, of which 3 were waited for; matrix products, arithmetic and copies ran while one was open for 13% of the time, Pallas kernels for 0%

commit v1 on v0

--- a/solution.py
+++ b/solution.py
@@ -1,8 +1,16 @@
+import functools
 import math
 import jax
 import jax.numpy as jnp
 from jax import lax
 from jax.sharding import PartitionSpec as P
+
+
+def switch_vector(block_here, dev_axis):
+    return jnp.sum(lax.all_gather(block_here, dev_axis), 0)
+
+
+divide_the_numbers = functools.partial(switch_vector, dev_axis="dev")
 
 
 def passed_along(block, axis, distance):
@@ -130,7 +138,7 @@
     local = own - group_index * owners
     local_range = jnp.arange(owners, dtype=jnp.int32)
     member = (local_range[:, None] == local[None, :]).astype(jnp.bfloat16)
-    sums = lax.psum(jnp.dot(member, documents, preferred_element_type=jnp.float32), "dev")
+    sums = divide_the_numbers(jnp.dot(member, documents, preferred_element_type=jnp.float32))
     own_sizes = lax.dynamic_slice_in_dim(sizes, group_index * owners, owners)
     means = sums / own_sizes.astype(jnp.float32)[:, None]
     centre = jnp.dot(

time: 227 us -> 195 us (0.86)
  waiting for transfers between devices: 169 us -> 137 us
    psum x1 -> x0, waiting for transfers between devices: 57.5 us -> none  [gathered(): lax.psum(jnp.dot(member, documents, preferred_element_type=jnp.float32),...]
    all_gather x0 -> x1, waiting for transfers between devices: none -> 24.8 us  [switch_vector(): return jnp.sum(lax.all_gather(block_here, dev_axis), 0)]
  transfers between devices with their start and end apart: 6 -> 6, of which waited for: 3 -> 3; matrix products, arithmetic and copies ran while one was open for 13% -> 15% of each run, Pallas kernels for 0% -> 0%
where the time goes in v1:
time: 195 us
  waiting for transfers between devices  137 us (70%)
  matrix products  32.4 us (17%)
  between operations  13.5 us (7%)
  starting transfers between devices  5.7 us (3%)
  other arithmetic  5.27 us (3%)
    all_gather x1, waiting for transfers between devices, gathered(): keys = lax.all_gather(unit_rows, 'dev', axis=0, tiled=True)  77.8 us
    ppermute x4, waiting for transfers between devices, passed_along(): return lax.ppermute(block, axis, route)  34 us
    dot_general x3, matrix products, partial(): jnp.einsum('qe,ke->qk', queries, keys, preferred_element_type=jnp.float32)  28 us
    all_gather x1, waiting for transfers between devices, switch_vector(): return jnp.sum(lax.all_gather(block_here, dev_axis), 0)  24.8 us
    ppermute x4, starting transfers between devices, passed_along(): return lax.ppermute(block, axis, route)  5.65 us
  transfers between devices with their start and end apart: 6, of which 3 were waited for; matrix products, arithmetic and copies ran while one was open for 15% of the time, Pallas kernels for 0%

profile of v1, /device:TPU:0, one launch (start us, length us, event | category | flops | bytes accessed | tf_op | source)
XLA Modules:
  0.0 195.0 jit_solution(17361632254989044931)
XLA Ops:
  6.5 0.0 copy-start.2
  6.5 0.0 all-gather.6.cloned.1.call-start
  6.5 0.9 broadcast_subtract_fusion
  7.4 0.0 copy-start.1
  7.4 2.5 %fusion.13 = f32[8,4096]{1,0:T(8,128)} fusion(bf16[192,4096]{1,0:T(8,128)(2,1)} %param.4, s32[192]{0:T(256)S(1)} %get-tuple-element.15), kind=kOutput, calls=%fused_computation.45 | convolution fusion | flops 12584448 | bytes 1704704 | tf_op jit(solution)/shard_map/dot_general | solution.py:141
  9.9 0.0 all-gather.6.cloned.1.call-update
  9.9 0.0 all-gather.4.cloned.1.call-start
  10.0 0.0 copy-done.2
  10.0 0.2 convert_reduce_fusion
  10.2 0.1 dynamic-slice_convert_fusion
  10.3 24.8 %all-gather.6.cloned.1.call-done = f32[64,4096]{1,0:T(8,128)} async-done(((f32[8,4096]{1,0:T(8,128)}), f32[64,4096]{1,0:T(8,128)}) %all-gather.6.cloned.1.call-update) | async-done | bytes 1048592 | tf_op jit(solution)/shard_map/all_gather | solution.py:10
  35.1 1.3 bitcast_reduce_fusion
  36.3 0.0 copy-done.1
  36.4 1.9 multiply_reduce_fusion
  38.2 1.5 multiply_convert_fusion
  39.8 0.0 copy-start
  39.8 0.0 copy-start.3
  39.8 0.0 copy-start.4
  39.8 0.0 all-gather.4.cloned.1.call-update
  39.8 1.4 copy-done
  41.2 2.4 %collective-permute-start.2 = (bf16[192,4096]{1,0:T(8,128)(2,1)S(1)}, bf16[192,4096]{1,0:T(8,128)(2,1)S(1)}, u32[]{:S(2)}, u32[]{:S(2)}) collective-permute-start(bf16[192,4096]{1,0:T(8,128)(2,1)S(1)} %copy-done), channel_id=1, source_target_pairs={{8,0},{16,8},{24,16},{0,24},{9,1},{17,9},{25,17},{1,25},{10,2},{18... | collective-permute-start | bytes 4718600 | tf_op jit(solution)/shard_map/ppermute | solution.py:19
  43.6 0.1 dynamic_slice.16
  43.6 0.0 copy-done.3
  43.6 0.1 select_reduce_fusion.3
  43.7 0.1 select_reduce_fusion.5
  43.8 0.0 copy-done.4
  43.8 0.1 select_reduce_fusion.4
  43.9 0.1 collective-permute-start
  44.0 0.2 select_reduce_fusion.12
  44.3 0.1 select_reduce_fusion.8
  44.4 0.1 select_reduce_fusion
  44.5 34.0 %collective-permute-done.2 = bf16[192,4096]{1,0:T(8,128)(2,1)S(1)} collective-permute-done((bf16[192,4096]{1,0:T(8,128)(2,1)S(1)}, bf16[192,4096]{1,0:T(8,128)(2,1)S(1)}, u32[]{:S(2)}, u32[]{:S(2)}) %collective-permute-start.2) | collective-permute-done | bytes 1572896 | tf_op jit(solution)/shard_map/ppermute | solution.py:19
  78.4 77.8 %all-gather.4.cloned.1.call-done = bf16[1536,4096]{1,0:T(8,128)(2,1)} async-done(((bf16[192,4096]{1,0:T(8,128)(2,1)}), bf16[1536,4096]{1,0:T(8,128)(2,1)}) %all-gather.4.cloned.1.call-update) | async-done | bytes 12582928 | tf_op jit(solution)/shard_map/all_gather | solution.py:155
  156.3 9.1 %fusion.8 = f32[192]{0:T(256)S(1)} fusion(bf16[192,4096]{1,0:T(8,128)(2,1)S(1)} %collective-permute-done.2, bf16[1536,4096]{1,0:T(8,128)(2,1)} %all-gather.4.cloned.1.call-done, f32[192]{0:T(256)S(1)} %get-tuple-element.9, f32[1536]{0:T(1024)S(1)} %select_reduce_fusion, s32[1536]{0:T(1024)S(1)} %dynamic_slice.16, s32[192]{0:T(256)S(1)} %select_reduce_fusion.3), kind=kOutput, calls=%fused_computation.14 | convolution fusion | flops 2417688320 | bytes 14170368 | tf_op jit(solution)/shard_map/qe,ke->qk/dot_general | solution.py:160
  165.3 1.5 collective-permute-start.3
  166.9 0.0 collective-permute-done
  166.9 9.6 %fusion.7 = f32[192]{0:T(256)S(1)} fusion(bf16[192,4096]{1,0:T(8,128)(2,1)} %collective-permute-done, bf16[1536,4096]{1,0:T(8,128)(2,1)} %all-gather.4.cloned.1.call-done, f32[192]{0:T(256)S(1)} %get-tuple-element.8, f32[1536]{0:T(1024)S(1)} %select_reduce_fusion, s32[1536]{0:T(1024)S(1)} %dynamic_slice.16, s32[192]{0:T(256)S(1)} %select_reduce_fusion.5), kind=kOutput, calls=%fused_computation.13 | convolution fusion | flops 2417688320 | bytes 14170368 | tf_op jit(solution)/shard_map/qe,ke->qk/dot_general | solution.py:160
  176.4 1.7 collective-permute-start.1
  178.1 9.4 %fusion.6 = f32[192]{0:T(256)S(1)} fusion(bf16[192,4096]{1,0:T(8,128)(2,1)S(1)} %copy-done, bf16[1536,4096]{1,0:T(8,128)(2,1)} %all-gather.4.cloned.1.call-done, f32[1536]{0:T(1024)S(1)} %select_reduce_fusion, f32[192]{0:T(256)S(1)} %get-tuple-element.10, s32[192]{0:T(256)S(1)} %iota_add_fusion, s32[1536]{0:T(1024)S(1)} %dynamic_slice.16, ...), kind=kOutput, calls=%fused_computation.12 | convolution fusion | flops 2419457792 | bytes 14172672 | tf_op jit(solution)/shard_map/qe,ke->qk/dot_general | solution.py:160
  187.5 0.0 collective-permute-done.3
  187.5 0.0 collective-permute-done.1
  187.5 0.6 fusion.16
  (4 shorter events, 0.0 us)
Async XLA Ops:
  6.5 3.5 %copy-start.2 = (s32[6144]{0:T(1024)S(1)}, s32[6144]{0:T(1024)}, u32[]{:S(2)}) copy-start(s32[6144]{0:T(1024)} %param.5) | copy-start | bytes 73732
  6.5 28.5 %all-gather.6.cloned.1.call-start = ((), (), s32[]{:S(2)}) async-start(), calls=%async_computation.1 | async-start | bytes 1179648 | tf_op jit(solution)/shard_map/all_gather | solution.py:10
  7.4 28.9 %copy-start.1 = (bf16[192,4096]{1,0:T(8,128)(2,1)S(1)}, bf16[192,4096]{1,0:T(8,128)(2,1)}, u32[]{:S(2)}) copy-start(bf16[192,4096]{1,0:T(8,128)(2,1)} %param.4) | copy-start | bytes 4718596
  9.9 146.3 %all-gather.4.cloned.1.call-start = ((), (), s32[]{:S(2)}) async-start(), calls=%async_computation | async-start | bytes 14155776 | tf_op jit(solution)/shard_map/all_gather | solution.py:155
  39.8 1.4 copy-start
  39.8 3.9 %copy-start.3 = (s32[32,4]{0,1:T(4,128)S(1)}, s32[32,4]{0,1:T(4,128)}, u32[]{:S(2)}) copy-start(s32[32,4]{0,1:T(4,128)} %param.6) | copy-start | bytes 1540
  39.8 4.1 %copy-start.4 = (f32[32]{0:T(128)S(1)}, f32[32]{0:T(128)}, u32[]{:S(2)}) copy-start(f32[32]{0:T(128)} %param.7) | copy-start | bytes 388
  41.2 37.3 %collective-permute-start.2 = (bf16[192,4096]{1,0:T(8,128)(2,1)S(1)}, bf16[192,4096]{1,0:T(8,128)(2,1)S(1)}, u32[]{:S(2)}, u32[]{:S(2)}) collective-permute-start(bf16[192,4096]{1,0:T(8,128)(2,1)S(1)} %copy-done), channel_id=1, source_target_pairs={{8,0},{16,8},{24,16},{0,24},{9,1},{17,9},{25,17},{1,25},{10,2},{18... | collective-permute-start | bytes 4718600 | tf_op jit(solution)/shard_map/ppermute | solution.py:19
  43.9 122.9 %collective-permute-start = (bf16[192,4096]{1,0:T(8,128)(2,1)S(1)}, bf16[192,4096]{1,0:T(8,128)(2,1)}, u32[]{:S(2)}, u32[]{:S(2)}) collective-permute-start(bf16[192,4096]{1,0:T(8,128)(2,1)S(1)} %copy-done), channel_id=1, source_target_pairs={{24,0},{0,8},{8,16},{16,24},{25,1},{1,9},{9,17},{17,25},{26,2},{2,... | collective-permute-start | bytes 4718600 | tf_op jit(solution)/shard_map/ppermute | solution.py:19
  165.3 22.2 %collective-permute-start.3 = (f32[192]{0:T(256)S(1)}, f32[192]{0:T(256)S(1)}, u32[]{:S(2)}, u32[]{:S(2)}) collective-permute-start(f32[192]{0:T(256)S(1)} %fusion.8), channel_id=1, source_target_pairs={{24,0},{0,8},{8,16},{16,24},{25,1},{1,9},{9,17},{17,25},{26,2},{2,... | collective-permute-start | bytes 2312 | tf_op jit(solution)/shard_map/ppermute | solution.py:19
  176.4 11.1 %collective-permute-start.1 = (f32[192]{0:T(256)S(1)}, f32[192]{0:T(256)S(1)}, u32[]{:S(2)}, u32[]{:S(2)}) collective-permute-start(f32[192]{0:T(256)S(1)} %fusion.7), channel_id=1, source_target_pairs={{8,0},{16,8},{24,16},{0,24},{9,1},{17,9},{25,17},{1,25},{10,2},{18... | collective-permute-start | bytes 2312 | tf_op jit(solution)/shard_map/ppermute | solution.py:19
Sparse Core Ops, SparseCore 0:
  10.1 24.9 all-gather.5
  39.9 116.3 all-gather.3
